TPU v7x, 16 devices: a whole 2x2x2 slice. The times are simulated.
16 devices in a mesh: cz: 2 (over z), cy: 2 (over y), cx: 4 (over x, core).
Axes of the slice: x: 2, y: 2, z: 2, core: 2. Of those that a mesh axis runs over, the one named last changes fastest.
Arguments:
- x: bfloat16 [768, 3072], P(('cx', 'cz'), 'cy')
- w1: bfloat16 [3072, 12288], P('cy', ('cz', 'cx'))
- w2: bfloat16 [12288, 3072], P('cz', ('cy', 'cx'))
Outputs:
- output: bfloat16 [768, 3072], P(('cx', 'cz'), 'cy')
All inputs are finite; a program needn't handle non-finite values.
Results may differ from a plain program's by a relative error of at most 0.0115084.
Values are sent between devices in bfloat16 or wider.
A program may use at most 1 GiB of HBM per device.

v0:
```python
import jax
import jax.numpy as jnp
from jax import lax
from jax.sharding import PartitionSpec as P


def solution(mesh):
    def body(x, w1, w2):
        xg = lax.all_gather(x, "cz", axis=0, tiled=True)
        w1g = lax.all_gather(w1, "cx", axis=1, tiled=True)
        cp = jnp.dot(xg, w1g, preferred_element_type=jnp.float32)
        c = lax.psum_scatter(cp, "cy", scatter_dimension=0, tiled=True).astype(jnp.bfloat16)
        h = jax.nn.gelu(c.astype(jnp.float32), approximate=True).astype(jnp.bfloat16)
        hg = lax.all_gather(h, "cy", axis=0, tiled=True)
        w2g = lax.all_gather(w2, "cx", axis=1, tiled=True)
        zp = jnp.dot(hg, w2g, preferred_element_type=jnp.float32)
        return lax.psum_scatter(zp, "cz", scatter_dimension=0, tiled=True).astype(jnp.bfloat16)

    return jax.shard_map(
        body,
        mesh=mesh,
        in_specs=(P(("cx", "cz"), "cy"), P("cy", ("cz", "cx")), P("cz", ("cy", "cx"))),
        out_specs=P(("cx", "cz"), "cy"),
        check_vma=False,
    )
```

profile of v0, /device:TPU:0, one launch (start us, length us, event | category | flops | bytes accessed | tf_op | source)
XLA Modules:
  0.0 397.4 jit_solution(15499400953833279737)
XLA Ops:
  6.5 0.0 all-gather.4.cloned.1.call-start
  6.5 0.0 copy-start
  6.5 0.7 all-gather.4.cloned.1.call-update
  7.3 0.0 reduce-scatter.3.cloned.1.call-start
  7.3 0.2 copy-done
  7.5 11.0 %all_gather.12 = bf16[192,1536]{1,0:T(8,128)(2,1)S(1)} all-gather(bf16[96,1536]{1,0:T(8,128)(2,1)S(1)} %copy-done), channel_id=1, replica_groups=mesh['cz'=2,'cy'=2,'cx'=4] {'cz'}, dimensions={0}, use_global_device_ids=true | all-gather | bytes 884736 | tf_op jit(solution)/shard_map/all_gather | solution.py:9
  18.5 112.2 %all-gather.4.cloned.1.call-done = bf16[1536,6144]{1,0:T(8,128)(2,1)} async-done(((bf16[1536,1536]{1,0:T(8,128)(2,1)}), bf16[1536,6144]{1,0:T(8,128)(2,1)}) %all-gather.4.cloned.1.call-update) | async-done | bytes 18874384 | tf_op jit(solution)/shard_map/all_gather | solution.py:10
  130.7 12.4 %fusion.6 = f32[192,6144]{1,0:T(8,128)} fusion(bf16[192,1536]{1,0:T(8,128)(2,1)S(1)} %all_gather.12, bf16[1536,6144]{1,0:T(8,128)(2,1)} %all-gather.4.cloned.1.call-done), kind=kOutput, calls=%fused_computation.10 | convolution fusion | flops 3623878656 | bytes 24182784 | tf_op jit(solution)/shard_map/dot_general | solution.py:11
  143.1 0.0 reduce-scatter.3.cloned.1.call-update
  143.1 0.0 all-gather.8.cloned.1.call-start
  143.1 0.7 all-gather.8.cloned.1.call-update
  143.8 0.0 all-gather.6.cloned.1.call-start
  143.9 57.5 %reduce-scatter.3.cloned.1.call-done = f32[96,6144]{1,0:T(8,128)} async-done(((f32[192,6144]{1,0:T(8,128)}), f32[96,6144]{1,0:T(8,128)}) %reduce-scatter.3.cloned.1.call-update) | async-done | bytes 2359312 | tf_op jit(solution)/shard_map/reduce_scatter | solution.py:12
  201.3 3.5 fusion.5
  204.8 0.0 all-gather.6.cloned.1.call-update
  204.8 0.0 reduce-scatter.5.cloned.1.call-start
  204.9 116.7 %all-gather.8.cloned.1.call-done = bf16[6144,1536]{1,0:T(8,128)(2,1)} async-done(((bf16[6144,384]{1,0:T(8,128)(2,1)}), bf16[6144,1536]{1,0:T(8,128)(2,1)}) %all-gather.8.cloned.1.call-update) | async-done | bytes 18874384 | tf_op jit(solution)/shard_map/all_gather | solution.py:15
  321.6 35.5 %all-gather.6.cloned.1.call-done = bf16[192,6144]{1,0:T(8,128)(2,1)} async-done(((bf16[96,6144]{1,0:T(8,128)(2,1)}), bf16[192,6144]{1,0:T(8,128)(2,1)}) %all-gather.6.cloned.1.call-update) | async-done | bytes 2359312 | tf_op jit(solution)/shard_map/all_gather | solution.py:14
  357.1 12.0 %fusion.7 = f32[192,1536]{1,0:T(8,128)} fusion(bf16[192,6144]{1,0:T(8,128)(2,1)} %all-gather.6.cloned.1.call-done, bf16[6144,1536]{1,0:T(8,128)(2,1)} %all-gather.8.cloned.1.call-done), kind=kOutput, calls=%fused_computation.11 | convolution fusion | flops 3623878656 | bytes 22413312 | tf_op jit(solution)/shard_map/dot_general | solution.py:16
  369.1 0.0 reduce-scatter.5.cloned.1.call-update
  369.1 20.0 %reduce-scatter.5.cloned.1.call-done = f32[96,1536]{1,0:T(8,128)} async-done(((f32[192,1536]{1,0:T(8,128)}), f32[96,1536]{1,0:T(8,128)}) %reduce-scatter.5.cloned.1.call-update) | async-done | bytes 589840 | tf_op jit(solution)/shard_map/reduce_scatter | solution.py:17
  389.1 1.8 convert_element_type.15
Async XLA Ops:
  6.5 124.1 %all-gather.4.cloned.1.call-start = ((), (), s32[]{:S(2)}) async-start(), calls=%async_computation.2 | async-start | bytes 23592960 | tf_op jit(solution)/shard_map/all_gather | solution.py:10
  6.5 1.0 copy-start
  7.3 194.1 %reduce-scatter.3.cloned.1.call-start = ((), (), s32[]{:S(2)}) async-start(), calls=%async_computation.3 | async-start | bytes 7077888 | tf_op jit(solution)/shard_map/reduce_scatter | solution.py:12
  143.1 178.5 %all-gather.8.cloned.1.call-start = ((), (), s32[]{:S(2)}) async-start(), calls=%async_computation.5 | async-start | bytes 23592960 | tf_op jit(solution)/shard_map/all_gather | solution.py:15
  143.8 213.2 %all-gather.6.cloned.1.call-start = ((), (), s32[]{:S(2)}) async-start(), calls=%async_computation.4 | async-start | bytes 3538944 | tf_op jit(solution)/shard_map/all_gather | solution.py:14
  204.8 184.2 %reduce-scatter.5.cloned.1.call-start = ((), (), s32[]{:S(2)}) async-start(), calls=%async_computation.6 | async-start | bytes 1769472 | tf_op jit(solution)/shard_map/reduce_scatter | solution.py:17
Sparse Core Ops, SparseCore 0:
  8.9 121.7 all-gather.3
  143.2 58.0 reduce-scatter.2
  202.9 118.6 all-gather.7
  323.0 34.0 all-gather.5
  369.2 19.8 reduce-scatter.4
where the time goes:
time: 398 us; the launch traced here: 397 us
  waiting for transfers between devices  343 us (86%)
  matrix products  24.4 us (6%)
  between operations  13.1 us (3%)
  blocking collectives  11 us (3%)
  other arithmetic  5.28 us (1%)
    all_gather x1, waiting for transfers between devices, body(): w2g = lax.all_gather(w2, 'cx', axis=1, tiled=True)  117 us
    all_gather x1, waiting for transfers between devices, body(): w1g = lax.all_gather(w1, 'cx', axis=1, tiled=True)  112 us
    reduce_scatter x1, waiting for transfers between devices, body(): lax.psum_scatter(cp, 'cy', scatter_dimension=0, tiled=True)  57.5 us
    all_gather x1, waiting for transfers between devices, body(): hg = lax.all_gather(h, 'cy', axis=0, tiled=True)  35.5 us
    reduce_scatter x1, waiting for transfers between devices, body(): lax.psum_scatter(zp, 'cz', scatter_dimension=0, tiled=True)  20 us
    dot_general x1, matrix products, body(): cp = jnp.dot(xg, w1g, preferred_element_type=jnp.float32)  12.4 us
    dot_general x1, matrix products, body(): zp = jnp.dot(hg, w2g, preferred_element_type=jnp.float32)  12 us
    all_gather x1, blocking collectives, body(): xg = lax.all_gather(x, 'cz', axis=0, tiled=True)  11 us
  transfers between devices with their start and end apart: 5, of which 5 were waited for; matrix products, arithmetic and copies ran while one was open for 1% of the time, Pallas kernels for 0%

commit v1 on v0

v1 whole, which is shorter than its diff:
```python
import functools

import jax
import jax.numpy as jnp
from jax import lax
from jax.experimental import pallas as pl
from jax.experimental.pallas import tpu as pltpu
from jax.sharding import PartitionSpec as P

MESH = pl.DeviceIdType.MESH
R = 48
Q = 96 // R
S = 8 * Q
AHEAD = 1
FWD_X = 1
FWD_DIAG = 2 * Q


def gelu(c):
    return 0.5 * c * (1.0 + jnp.tanh(0.7978845608028654 * (c + 0.044715 * (c * c * c))))


def kernel(x_ref, w1_ref, w2_ref, out_ref, xg, w1v, w2v, ps, pr, hb, zacc, zr, zo, zfin,
           load_sem, x_send, x_sem, xc_sem, p_send, p_sem, h_send, hy_sem, hx_sem, hxd_sem,
           hc_sem, z_send, z_sem, f_send, f_sem):
    cz, cy, cx = lax.axis_index("cz"), lax.axis_index("cy"), lax.axis_index("cx")
    core = lax.rem(cx, 2)
    chip = lax.div(cx, 2)
    cxn = lax.rem(cx + 2, 4)
    cxp = cx + 1 - 2 * core
    y_dev = (cz, 1 - cy, cx)
    z_dev = (1 - cz, cy, cx)
    x_dev = (cz, cy, cxn)
    c_dev = (cz, cy, cxp)
    xc_dev = (cz, cy, lax.rem(cxp + 2, 4))

    def remote(src, dst, send, recv, dev):
        return pltpu.make_async_remote_copy(
            src_ref=src, dst_ref=dst, send_sem=send, recv_sem=recv, device_id=dev, device_id_type=MESH)

    def token(s, xx):
        seg, sub = lax.div(s, Q), lax.rem(s, Q)
        kind = lax.div(seg, 2)
        tx = jnp.where(kind < 2, xx, 1 - xx)
        tz = jnp.where((kind == 0) | (kind == 3), cz, 1 - cz)
        tcx = 2 * tx + lax.rem(seg, 2)
        return tcx, tz, sub

    def index(s, xx):
        tcx, tz, sub = token(s, xx)
        return (tcx * 2 + tz) * Q + sub

    def block(tcx, tz):
        return xg.at[pl.ds((tcx * 2 + tz) * Q, Q)]

    def x_copy(kind, tcx, tz, dev):
        return remote(block(tcx, tz), block(tcx, tz), x_send.at[kind], x_sem.at[kind], dev)

    def xc_copy(kind, tcx, tz):
        return remote(block(tcx, tz), block(tcx, tz), x_send.at[3 + kind], xc_sem.at[kind], c_dev)

    barrier = pltpu.get_barrier_semaphore()
    for dev in (y_dev, z_dev, x_dev, c_dev, xc_dev):
        pl.semaphore_signal(barrier, inc=1, device_id=dev, device_id_type=MESH)
    loads = [
        pltpu.make_async_copy(x_ref, block(cx, cz), load_sem.at[0]),
        pltpu.make_async_copy(w1_ref.at[:, pl.ds(pl.multiple_of((1 - cy) * 768, 128), 768)], w1v.at[0], load_sem.at[1]),
        pltpu.make_async_copy(w1_ref.at[:, pl.ds(pl.multiple_of(cy * 768, 128), 768)], w1v.at[1], load_sem.at[2]),
        pltpu.make_async_copy(w2_ref, w2v, load_sem.at[3]),
    ]
    for load in loads:
        load.start()
    loads[0].wait()
    pl.semaphore_wait(barrier, 5)

    xc_copy(0, cx, cz).start()
    x_copy(0, cx, cz, x_dev).start()
    x_copy(1, cx, cz, z_dev).start()
    loads[1].wait()

    def p_copy(s):
        return remote(ps.at[s], pr.at[s], p_send, p_sem.at[s], y_dev)

    def send_partial(s):
        tcx, tz, sub = token(s, chip)
        kind = lax.div(s, 2 * Q)

        @pl.when((sub == 0) & (lax.rem(tcx, 2) != core))
        def _():
            xc_copy(kind, tcx, tz).wait_recv()

        ps[s] = jnp.dot(xg[(tcx * 2 + tz) * Q + sub], w1v[0], preferred_element_type=jnp.float32)
        p_copy(s).start()

    def h_copy(slot, t, b, recv, dev):
        return remote(hb.at[t, b], hb.at[t, b], h_send.at[slot], recv, dev)

    def own_y(s):
        return h_copy(0, index(s, chip), cx * 2 + cy, hy_sem.at[s], y_dev)

    def own_x(s):
        return h_copy(1, index(s, chip), cx * 2 + cy, hx_sem.at[s], x_dev)

    def own_c(s):
        return h_copy(2, index(s, chip), cx * 2 + cy, hc_sem.at[0, s], c_dev)

    def y_to_x(s):
        return h_copy(3, index(s, chip), cx * 2 + 1 - cy, hxd_sem.at[s], x_dev)

    def y_to_c(s):
        return h_copy(4, index(s, chip), cx * 2 + 1 - cy, hc_sem.at[1, s], c_dev)

    def x_to_c(s):
        return h_copy(5, index(s, 1 - chip), cxn * 2 + cy, hc_sem.at[2, s], c_dev)

    def d_to_c(s):
        return h_copy(6, index(s, 1 - chip), cxn * 2 + 1 - cy, hc_sem.at[3, s], c_dev)

    def make_h(s):
        t = index(s, chip)
        keep = jnp.dot(xg[t], w1v[1], preferred_element_type=jnp.float32)
        p_copy(s).wait_recv()
        c = (keep + pr[s]).astype(jnp.bfloat16).astype(jnp.float32)
        hb[t, cx * 2 + cy] = gelu(c).astype(jnp.bfloat16)
        own_y(s).start()
        own_x(s).start()
        own_c(s).start()

    def layer2(t, xx):
        acc = zacc[t]
        for j in range(4):
            b = xx * 4 + j
            acc += jnp.dot(hb[t, b], w2v[b], preferred_element_type=jnp.float32)
        return acc

    def z_copy(t, tcx, sub):
        return remote(zacc.at[t], zr.at[tcx * Q + sub], z_send, z_sem.at[tcx * Q + sub], z_dev)

    def f_copy(tcx, sub, dev):
        return remote(zo.at[tcx * Q + sub], zfin.at[sub, cx], f_send, f_sem.at[sub, cx], dev)

    def finish(s, xx, local):
        tcx, tz, sub = token(s, xx)
        t = (tcx * 2 + tz) * Q + sub
        kind = lax.div(s, 2 * Q)
        acc = layer2(t, xx)

        @pl.when(kind < 3)
        def _():
            zacc[t] = acc

        @pl.when(kind == 2)
        def _():
            z_copy(t, tcx, sub).start()

        @pl.when(kind == 3)
        def _():
            k = tcx * Q + sub
            remote(zacc.at[t], zr.at[k], z_send, z_sem.at[k], z_dev).wait_recv()
            z = (acc + zr[k]).astype(jnp.bfloat16)
            if local:
                @pl.when(tcx == cx)
                def _():
                    zfin[sub, cx] = z

                @pl.when(tcx != cx)
                def _():
                    zo[k] = z
                    f_copy(tcx, sub, c_dev).start()
            else:
                zo[k] = z
                f_copy(tcx, sub, (cz, cy, tcx)).start()

    for s in range(AHEAD):
        send_partial(s)
    zacc[...] = jnp.zeros_like(zacc)
    loads[2].wait()
    loads[3].wait()

    def body(i, _):
        @pl.when(i + AHEAD < S)
        def _():
            send_partial(i + AHEAD)

        @pl.when(i < S)
        def _():
            make_h(i)

        @pl.when(i == FWD_X)
        def _():
            x_copy(1, cx, 1 - cz, z_dev).wait_recv()
            xc_copy(1, cx, 1 - cz).start()
            x_copy(0, cxn, cz, x_dev).wait_recv()
            x_copy(2, cxn, cz, z_dev).start()
            xc_copy(3, cxn, cz).start()

        @pl.when(i == FWD_DIAG)
        def _():
            x_copy(2, cxn, 1 - cz, z_dev).wait_recv()
            xc_copy(2, cxn, 1 - cz).start()

        @pl.when((i >= 1) & (i < S + 1))
        def _():
            s = i - 1
            own_y(s).wait_recv()
            y_to_x(s).start()
            y_to_c(s).start()
            own_x(s).wait_recv()
            x_to_c(s).start()

        @pl.when((i >= 2) & (i < S + 2))
        def _():
            s = i - 2
            own_c(s).wait_recv()
            y_to_c(s).wait_recv()
            finish(s, chip, False)
            y_to_x(s).wait_recv()
            d_to_c(s).start()

        @pl.when(i >= 3)
        def _():
            s = i - 3
            x_to_c(s).wait_recv()
            d_to_c(s).wait_recv()
            finish(s, 1 - chip, True)

        return 0

    lax.fori_loop(0, S + 3, body, 0)

    for sub in range(Q):
        for j in range(4):
            @pl.when(j != cx)
            def _():
                remote(zo.at[sub], zfin.at[sub, j], f_send, f_sem.at[sub, j], c_dev).wait_recv()
            out_ref[sub, :, j * 384:(j + 1) * 384] = zfin[sub, j]

    for kind, (tcx, tz, dev) in enumerate(((cx, cz, x_dev), (cx, cz, z_dev), (cxn, cz, z_dev))):
        x_copy(kind, tcx, tz, dev).wait_send()
    for kind, (tcx, tz) in enumerate(((cx, cz), (cx, 1 - cz), (cxn, 1 - cz), (cxn, cz))):
        xc_copy(kind, tcx, tz).wait_send()
    pltpu.make_async_copy(ps, pr, p_send).wait()
    for slot in range(7):
        half = hb.at[pl.ds(0, S), 0]
        pltpu.make_async_copy(half, half, h_send.at[slot]).wait()
    half = zacc.at[pl.ds(0, 4 * Q)]
    pltpu.make_async_copy(half, zr, z_send).wait()
    part = zo.at[pl.ds(0, 3 * Q)]
    pltpu.make_async_copy(part, part, f_send).wait()


def solution(mesh):
    def body(x, w1, w2):
        bf16, f32 = jnp.bfloat16, jnp.float32
        dma = pltpu.SemaphoreType.DMA
        out = pl.pallas_call(
            kernel,
            out_shape=jax.ShapeDtypeStruct((Q, R, 1536), bf16),
            in_specs=[pl.BlockSpec(memory_space=pl.ANY)] * 3,
            out_specs=pl.BlockSpec(memory_space=pltpu.VMEM),
            scratch_shapes=[
                pltpu.VMEM((S, R, 1536), bf16),
                pltpu.VMEM((2, 1536, 768), bf16),
                pltpu.VMEM((8, 768, 384), bf16),
                pltpu.VMEM((S, R, 768), f32),
                pltpu.VMEM((S, R, 768), f32),
                pltpu.VMEM((S, 8, R, 768), bf16),
                pltpu.VMEM((S, R, 384), f32),
                pltpu.VMEM((4 * Q, R, 384), f32),
                pltpu.VMEM((4 * Q, R, 384), bf16),
                pltpu.VMEM((Q, 4, R, 384), bf16),
                dma((4,)), dma((7,)), dma((3,)), dma((4,)), dma(()), dma((S,)), dma((7,)), dma((S,)), dma((S,)),
                dma((S,)), dma((4, S)), dma(()), dma((4 * Q,)), dma(()), dma((Q, 4)),
            ],
            compiler_params=pltpu.CompilerParams(
                collective_id=0, has_side_effects=True, vmem_limit_bytes=67_043_328),
        )(x.reshape(Q, R, 1536), w1, w2.reshape(8, 768, 384))
        return out.reshape(96, 1536)

    return jax.shard_map(
        body,
        mesh=mesh,
        in_specs=(P(("cx", "cz"), "cy"), P("cy", ("cz", "cx")), P("cz", ("cy", "cx"))),
        out_specs=P(("cx", "cz"), "cy"),
        check_vma=False,
    )
```

time: 398 us -> 94.8 us (0.24)
  waiting for transfers between devices: 343 us -> 0 us
  Pallas kernels: 0 us -> 93 us
  matrix products: 24.4 us -> 0 us
  between operations: 13.1 us -> 0.01 us
  blocking collectives: 11 us -> 0 us
  other arithmetic: 5.28 us -> 0 us
    all_gather x3 -> x0, waiting for transfers between devices: 264 us -> none  [the longest x1 117 us: body(): w2g = lax.all_gather(w2, 'cx', axis=1, tiled=True)]
    pallas_call x0 -> x1, Pallas kernels: none -> 93 us  [body(): pl.pallas_call(kernel, out_shape=jax.ShapeDtypeStruct((Q, R, 1536), bf16)...]
    reduce_scatter x2 -> x0, waiting for transfers between devices: 77.5 us -> none  [the longest x1 57.5 us: body(): lax.psum_scatter(cp, 'cy', scatter_dimension=0, tiled=True)]
    dot_general x2 -> x0, matrix products: 24.4 us -> none  [the longest x1 12.4 us: body(): cp = jnp.dot(xg, w1g, preferred_element_type=jnp.float32)]
    all_gather x1 -> x0, blocking collectives: 11 us -> none  [body(): xg = lax.all_gather(x, 'cz', axis=0, tiled=True)]
    convert_element_type x2 -> x0, other arithmetic: 5.28 us -> none  [the longest x1 3.47 us: body(): jax.nn.gelu(c.astype(jnp.float32), approximate=True).astype(jnp.bfloat16)]
  transfers between devices with their start and end apart: 5 -> 0, of which waited for: 5 -> 0; matrix products, arithmetic and copies ran while one was open for 1% -> 0% of each run, Pallas kernels for 0% -> 0%
where the time goes in v1:
time: 94.8 us; the launch traced here: 94.7 us
  Pallas kernels  93 us (98%)
  local copies, waits for them, and re-layouts  1.69 us (2%)
    pallas_call x1, Pallas kernels, body(): pl.pallas_call(kernel, out_shape=jax.ShapeDtypeStruct((Q, R, 1536), bf16)...  93 us

profile of v1, /device:TPU:0, one launch (start us, length us, event | category | flops | bytes accessed | tf_op | source)
XLA Modules:
  0.0 94.7 jit_solution(10345262994697834712)
XLA Ops:
  0.0 93.0 %shard_map.37 = bf16[2,48,1536]{2,1,0:T(8,128)(2,1)} custom-call(bf16[2,48,1536]{2,1,0:T(8,128)(2,1)} %bitcast.5, bf16[1536,1536]{1,0:T(8,128)(2,1)} %w1_ref.1, bf16[8,768,384]{2,1,0:T(8,128)(2,1)} %bitcast.3), custom_call_target="tpu_custom_call" | custom-call | tf_op jit(solution)/shard_map/pallas_call | solution.py:256
  93.0 1.7 %copy.5 = bf16[96,1536]{1,0:T(8,128)(2,1)} copy(bf16[96,1536]{1,0:T(8,128)(2,1)} %bitcast.4) | data formatting | bytes 589824

commit v2 on v1

v2 whole, which is shorter than its diff:
```python
import functools

import jax
import jax.numpy as jnp
from jax import lax
from jax.experimental import pallas as pl
from jax.experimental.pallas import tpu as pltpu
from jax.sharding import PartitionSpec as P

MESH = pl.DeviceIdType.MESH
R = 48
Q = 96 // R
S = 8 * Q
T = S - 2
PIECE = 16
N = R // PIECE
K = 8
FWD_X = 1
FWD_DIAG = 2 * Q


def gelu(c):
    return 0.5 * c * (1.0 + jnp.tanh(0.7978845608028654 * (c + 0.044715 * (c * c * c))))


def kernel(x_ref, w1_ref, w2_ref, out_ref, xg, w1v, w2v, ps, pr, kept, hb, zacc, zr, zo, zfin,
           load_sem, x_send, x_sem, xc_sem, p_send, p_sem, h_send, hy_sem, hx_sem, hd_sem,
           ca_sem, cb_sem, z_send, z_sem, f_send, f_sem):
    cz, cy, cx = lax.axis_index("cz"), lax.axis_index("cy"), lax.axis_index("cx")
    core = lax.rem(cx, 2)
    chip = lax.div(cx, 2)
    cxn = lax.rem(cx + 2, 4)
    cxp = cx + 1 - 2 * core
    y_dev = (cz, 1 - cy, cx)
    z_dev = (1 - cz, cy, cx)
    x_dev = (cz, cy, cxn)
    c_dev = (cz, cy, cxp)
    xc_dev = (cz, cy, lax.rem(cxp + 2, 4))

    def remote(src, dst, send, recv, dev):
        return pltpu.make_async_remote_copy(
            src_ref=src, dst_ref=dst, send_sem=send, recv_sem=recv, device_id=dev, device_id_type=MESH)

    def token(s, xx):
        seg, sub = lax.div(s, Q), lax.rem(s, Q)
        kind = lax.div(seg, 2)
        tx = jnp.where(kind < 2, xx, 1 - xx)
        tz = jnp.where((kind == 0) | (kind == 3), cz, 1 - cz)
        tcx = 2 * tx + lax.rem(seg, 2)
        return tcx, tz, sub

    def index(s, xx):
        tcx, tz, sub = token(s, xx)
        return (tcx * 2 + tz) * Q + sub

    def block(tcx, tz):
        return xg.at[pl.ds((tcx * 2 + tz) * Q, Q)]

    def x_copy(kind, tcx, tz, dev):
        return remote(block(tcx, tz), block(tcx, tz), x_send, x_sem.at[kind], dev)

    def xc_copy(kind, tcx, tz):
        return remote(block(tcx, tz), block(tcx, tz), x_send, xc_sem.at[kind], c_dev)

    def whole(s):
        return s, lax.rem(s, K), pl.ds(0, R)

    def pieces(s):
        return [(s, (T + (s - T) * N + p) % K, pl.ds(p * PIECE, PIECE)) for p in range(N)]

    def p_copy(m):
        s, q, rows = m
        return remote(ps.at[s, rows], pr.at[s, rows], p_send, p_sem.at[q], y_dev)

    def h_copy(t, b, rows, recv, dev):
        return remote(hb.at[t, b, rows], hb.at[t, b, rows], h_send, recv, dev)

    def own_y(m):
        s, q, rows = m
        return h_copy(index(s, chip), cx * 2 + cy, rows, hy_sem.at[q], y_dev)

    def own_x(m):
        s, q, rows = m
        return h_copy(index(s, chip), cx * 2 + cy, rows, hx_sem.at[q], x_dev)

    def y_to_x(m):
        s, q, rows = m
        return h_copy(index(s, chip), cx * 2 + 1 - cy, rows, hd_sem.at[q], x_dev)

    def pair_a(m):
        s, q, rows = m
        return h_copy(index(s, chip), pl.ds(cx * 2, 2), rows, ca_sem.at[q], c_dev)

    def pair_b(m):
        s, q, rows = m
        return h_copy(index(s, 1 - chip), pl.ds(cxn * 2, 2), rows, cb_sem.at[q], c_dev)

    def partial(s):
        tcx, tz, sub = token(s, chip)

        @pl.when((sub == 0) & (lax.rem(tcx, 2) != core))
        def _():
            xc_copy(lax.div(s, 2 * Q), tcx, tz).wait_recv()

        ps[s] = jnp.dot(xg[(tcx * 2 + tz) * Q + sub], w1v[0], preferred_element_type=jnp.float32)

    def keep(s):
        kept[...] = jnp.dot(xg[index(s, chip)], w1v[1], preferred_element_type=jnp.float32)

    def make_h(m):
        s, _, rows = m
        p_copy(m).wait_recv()
        c = (kept[rows] + pr[s, rows]).astype(jnp.bfloat16).astype(jnp.float32)
        hb[index(s, chip), cx * 2 + cy, rows] = gelu(c).astype(jnp.bfloat16)
        own_y(m).start()
        own_x(m).start()

    def layer2(t, xx):
        acc = zacc[t]
        for j in range(4):
            b = xx * 4 + j
            acc += jnp.dot(hb[t, b], w2v[b], preferred_element_type=jnp.float32)
        return acc

    def z_copy(t, k):
        return remote(zacc.at[t], zr.at[k], z_send, z_sem.at[k], z_dev)

    def f_copy(tcx, sub, dev):
        return remote(zo.at[tcx * Q + sub], zfin.at[sub, cx], f_send, f_sem, dev)

    def finish(s, xx, local):
        tcx, tz, sub = token(s, xx)
        t = (tcx * 2 + tz) * Q + sub
        k = tcx * Q + sub
        kind = lax.div(s, 2 * Q)
        acc = layer2(t, xx)

        @pl.when(kind < 3)
        def _():
            zacc[t] = acc

        @pl.when(kind == 2)
        def _():
            z_copy(t, k).start()

        @pl.when(kind == 3)
        def _():
            z_copy(t, k).wait_recv()
            z = (acc + zr[k]).astype(jnp.bfloat16)
            if local:
                @pl.when(tcx == cx)
                def _():
                    zfin[sub, cx] = z

                @pl.when(tcx != cx)
                def _():
                    zo[k] = z
                    f_copy(tcx, sub, c_dev).start()
            else:
                zo[k] = z
                f_copy(tcx, sub, (cz, cy, tcx)).start()

    def relay(m):
        own_y(m).wait_recv()
        y_to_x(m).start()
        pair_a(m).start()
        own_x(m).wait_recv()

    def relay_diag(m):
        y_to_x(m).wait_recv()
        pair_b(m).start()

    def near(s, ms):
        for m in ms:
            pair_a(m).wait_recv()
        finish(s, chip, False)

    def far(s, ms):
        for m in ms:
            pair_b(m).wait_recv()
        finish(s, 1 - chip, True)

    barrier = pltpu.get_barrier_semaphore()
    partners = (y_dev, z_dev, x_dev, c_dev, xc_dev)
    for dev in partners:
        pl.semaphore_signal(barrier, inc=1, device_id=dev, device_id_type=MESH)
    other = pl.multiple_of((1 - cy) * 768, 128)
    mine = pl.multiple_of(cy * 768, 128)
    x_load = pltpu.make_async_copy(x_ref, block(cx, cz), load_sem.at[0])
    first_loads = [
        pltpu.make_async_copy(w1_ref.at[:, pl.ds(other + j * 256, 256)], w1v.at[0, :, pl.ds(j * 256, 256)], load_sem.at[1 + j])
        for j in range(3)]
    keep_load = pltpu.make_async_copy(w1_ref.at[:, pl.ds(mine, 768)], w1v.at[1], load_sem.at[4])
    w2_load = pltpu.make_async_copy(w2_ref, w2v, load_sem.at[5])
    x_load.start()
    for load in first_loads:
        load.start()
    x_load.wait()
    pl.semaphore_wait(barrier, len(partners))
    xc_copy(0, cx, cz).start()
    x_copy(0, cx, cz, x_dev).start()
    x_copy(1, cx, cz, z_dev).start()

    @pl.when(core == 1)
    def _():
        xc_copy(0, cx - 1, cz).wait_recv()

    for j, load in enumerate(first_loads):
        load.wait()
        cols = pl.ds(j * 256, 256)
        ps[0, :, cols] = jnp.dot(xg[index(0, chip)], w1v[0, :, cols], preferred_element_type=jnp.float32)
    p_copy(whole(0)).start()
    keep_load.start()
    w2_load.start()
    zacc[...] = jnp.zeros_like(zacc)

    def body(i, _):
        partial(i + 1)
        p_copy(whole(i + 1)).start()

        @pl.when(i == 0)
        def _():
            keep_load.wait()

        keep(i)
        make_h(whole(i))

        @pl.when(i == FWD_X)
        def _():
            w2_load.wait()
            x_copy(1, cx, 1 - cz, z_dev).wait_recv()
            xc_copy(1, cx, 1 - cz).start()
            x_copy(0, cxn, cz, x_dev).wait_recv()
            x_copy(2, cxn, cz, z_dev).start()
            xc_copy(3, cxn, cz).start()

        @pl.when(i == FWD_DIAG)
        def _():
            x_copy(2, cxn, 1 - cz, z_dev).wait_recv()
            xc_copy(2, cxn, 1 - cz).start()

        @pl.when(i >= 1)
        def _():
            relay(whole(i - 1))

        @pl.when(i >= 2)
        def _():
            m = whole(i - 2)
            near(i - 2, [m])
            relay_diag(m)

        @pl.when(i >= 3)
        def _():
            far(i - 3, [whole(i - 3)])

        return 0

    lax.fori_loop(0, T - 1, body, 0)

    m = pieces(T) + pieces(T + 1)
    w = {s: whole(s) for s in range(T - 4, T)}
    partial(T)
    p_copy(m[0]).start()
    p_copy(m[1]).start()
    keep(T - 1)
    make_h(w[T - 1])
    p_copy(m[2]).start()
    relay(w[T - 2])
    near(T - 3, [w[T - 3]])
    relay_diag(w[T - 3])
    far(T - 4, [w[T - 4]])

    partial(T + 1)
    keep(T)
    make_h(m[0])
    p_copy(m[3]).start()
    relay(w[T - 1])
    near(T - 2, [w[T - 2]])
    relay_diag(w[T - 2])

    make_h(m[1])
    p_copy(m[4]).start()
    far(T - 3, [w[T - 3]])

    make_h(m[2])
    p_copy(m[5]).start()
    relay(m[0])
    keep(T + 1)
    near(T - 1, [w[T - 1]])
    relay_diag(w[T - 1])

    make_h(m[3])
    relay(m[1])
    far(T - 2, [w[T - 2]])

    make_h(m[4])
    relay(m[2])
    far(T - 1, [w[T - 1]])

    make_h(m[5])
    relay(m[3])
    near(T, m[:3])
    relay_diag(m[0])
    relay_diag(m[1])
    relay(m[4])
    relay(m[5])
    relay_diag(m[2])
    far(T, m[:3])
    near(T + 1, m[3:])
    for piece in m[3:]:
        relay_diag(piece)
    far(T + 1, m[3:])

    part = zo.at[pl.ds(0, 3 * Q)]
    pltpu.make_async_copy(part, part, f_sem).wait()
    for sub in range(Q):
        for j in range(4):
            out_ref[sub, :, j * 384:(j + 1) * 384] = zfin[sub, j]

    sent = xg.at[pl.ds(0, 7 * Q)]
    pltpu.make_async_copy(sent, sent, x_send).wait()
    pltpu.make_async_copy(ps, pr, p_send).wait()
    sent = hb.at[:, pl.ds(0, 7)]
    pltpu.make_async_copy(sent, sent, h_send).wait()
    pltpu.make_async_copy(zr, zr, z_send).wait()
    pltpu.make_async_copy(part, part, f_send).wait()


def solution(mesh):
    def body(x, w1, w2):
        bf16, f32 = jnp.bfloat16, jnp.float32
        dma = pltpu.SemaphoreType.DMA
        inputs = (x.reshape(Q, R, 1536), w1, w2.reshape(8, 768, 384))
        out = pl.pallas_call(
            kernel,
            out_shape=jax.ShapeDtypeStruct((Q, R, 1536), bf16),
            in_specs=[pl.BlockSpec(memory_space=pltpu.HBM)] * 3,
            out_specs=pl.BlockSpec(memory_space=pltpu.VMEM),
            scratch_shapes=[
                pltpu.VMEM((S, R, 1536), bf16),
                pltpu.VMEM((2, 1536, 768), bf16),
                pltpu.VMEM((8, 768, 384), bf16),
                pltpu.VMEM((S, R, 768), f32),
                pltpu.VMEM((S, R, 768), f32),
                pltpu.VMEM((R, 768), f32),
                pltpu.VMEM((S, 8, R, 768), bf16),
                pltpu.VMEM((S, R, 384), f32),
                pltpu.VMEM((4 * Q, R, 384), f32),
                pltpu.VMEM((4 * Q, R, 384), bf16),
                pltpu.VMEM((Q, 4, R, 384), bf16),
                dma((6,)), dma(()), dma((3,)), dma((4,)), dma(()), dma((K,)), dma(()), dma((K,)), dma((K,)),
                dma((K,)), dma((K,)), dma((K,)), dma(()), dma((4 * Q,)), dma(()), dma(()),
            ],
            compiler_params=pltpu.CompilerParams(
                collective_id=0, has_side_effects=True, vmem_limit_bytes=40 * 2**20),
        )(*(pltpu.with_memory_space_constraint(v, pltpu.HBM) for v in inputs))
        return out.reshape(96, 1536)

    return jax.shard_map(
        body,
        mesh=mesh,
        in_specs=(P(("cx", "cz"), "cy"), P("cy", ("cz", "cx")), P("cz", ("cy", "cx"))),
        out_specs=P(("cx", "cz"), "cy"),
        check_vma=False,
    )
```

time: 94.8 us -> 91.4 us (0.964)
  Pallas kernels: 93 us -> 90.5 us
  local copies, waits for them, and re-layouts: 1.69 us -> 0.72 us
    pallas_call x1, Pallas kernels: 93 us -> 90.5 us  [body(): pl.pallas_call(kernel, out_shape=jax.ShapeDtypeStruct((Q, R, 1536), bf16)...]
    unnamed x1, local copies, waits for them, and re-layouts: 1.69 us -> 0.72 us
where the time goes in v2:
time: 91.4 us; the launch traced here: 91.3 us
  Pallas kernels  90.5 us (99%)
    pallas_call x1, Pallas kernels, body(): pl.pallas_call(kernel, out_shape=jax.ShapeDtypeStruct((Q, R, 1536), bf16)...  90.5 us

profile of v2, /device:TPU:0, one launch (start us, length us, event | category | flops | bytes accessed | tf_op | source)
XLA Modules:
  0.0 91.3 jit_solution(2693803311995961213)
XLA Ops:
  0.0 90.5 %shard_map.37 = bf16[2,48,1536]{2,1,0:T(8,128)(2,1)S(1)} custom-call(bf16[2,48,1536]{2,1,0:T(8,128)(2,1)} %bitcast.5, bf16[1536,1536]{1,0:T(8,128)(2,1)} %w1_ref.1, bf16[8,768,384]{2,1,0:T(8,128)(2,1)} %bitcast.4), custom_call_target="tpu_custom_call" | custom-call | tf_op jit(solution)/shard_map/pallas_call | solution.py:334
  90.5 0.7 copy.5

commit v3 on v2

v3 whole, which is shorter than its diff:
```python
import functools

import jax
import jax.numpy as jnp
from jax import lax
from jax.experimental import pallas as pl
from jax.experimental.pallas import tpu as pltpu
from jax.sharding import PartitionSpec as P

MESH = pl.DeviceIdType.MESH
R = 48
Q = 96 // R
S = 8 * Q
T = S - 2
PIECE = 16
N = R // PIECE
K = 8
KX = 10
FWD_X = 1
FWD_DIAG = 2 * Q


def gelu(c):
    return 0.5 * c * (1.0 + jnp.tanh(0.7978845608028654 * (c + 0.044715 * (c * c * c))))


def kernel(x_ref, w1_ref, w2_ref, out_ref, xg, w1v, w2v, ps, pr, kept, hb, zacc, zr, zo, zfin,
           load_sem, x_send, x_sem, xc_sem, p_send, p_sem, h_send, hy_sem, hx_sem, hd_sem,
           ca_sem, cb_sem, z_send, z_sem, f_send, f_sem):
    cz, cy, cx = lax.axis_index("cz"), lax.axis_index("cy"), lax.axis_index("cx")
    core = lax.rem(cx, 2)
    chip = lax.div(cx, 2)
    cxn = lax.rem(cx + 2, 4)
    cxp = cx + 1 - 2 * core
    y_dev = (cz, 1 - cy, cx)
    z_dev = (1 - cz, cy, cx)
    x_dev = (cz, cy, cxn)
    c_dev = (cz, cy, cxp)
    xc_dev = (cz, cy, lax.rem(cxp + 2, 4))
    d_dev = (cz, 1 - cy, cxn)

    def remote(src, dst, send, recv, dev):
        return pltpu.make_async_remote_copy(
            src_ref=src, dst_ref=dst, send_sem=send, recv_sem=recv, device_id=dev, device_id_type=MESH)

    def token(s, xx, kk):
        seg, sub = lax.div(s, Q), lax.rem(s, Q)
        kind = lax.div(seg, 2)
        tx = jnp.where(kind < 2, xx, 1 - xx)
        tz = jnp.where((kind == 0) | (kind == 3), cz, 1 - cz)
        tcx = 2 * tx + jnp.where(kind == 0, lax.rem(seg + kk, 2), lax.rem(seg, 2))
        return tcx, tz, sub

    def index(s, xx, kk):
        tcx, tz, sub = token(s, xx, kk)
        return (tcx * 2 + tz) * Q + sub

    def block(tcx, tz):
        return xg.at[pl.ds((tcx * 2 + tz) * Q, Q)]

    def x_copy(kind, tcx, tz, dev):
        return remote(block(tcx, tz), block(tcx, tz), x_send, x_sem.at[kind], dev)

    def xc_copy(kind, tcx, tz):
        return remote(block(tcx, tz), block(tcx, tz), x_send, xc_sem.at[kind], c_dev)

    def whole(s):
        return s, s, pl.ds(0, R)

    def pieces(s):
        return [(s, T + (s - T) * N + p, pl.ds(p * PIECE, PIECE)) for p in range(N)]

    def p_copy(m):
        s, q, rows = m
        return remote(ps.at[s, rows], pr.at[s, rows], p_send, p_sem.at[lax.rem(q, K)], y_dev)

    def h_copy(t, b, rows, recv, dev):
        return remote(hb.at[t, b, rows], hb.at[t, b, rows], h_send, recv, dev)

    def own_y(m):
        s, q, rows = m
        return h_copy(index(s, chip, core), cx * 2 + cy, rows, hy_sem.at[lax.rem(q, K)], y_dev)

    def own_x(m):
        s, q, rows = m
        return h_copy(index(s, chip, core), cx * 2 + cy, rows, hx_sem.at[lax.rem(q, KX)], x_dev)

    def y_to_x(m):
        s, q, rows = m
        return h_copy(index(s, chip, core), cx * 2 + 1 - cy, rows, hd_sem.at[lax.rem(q, K)], x_dev)

    def own_d(m, j):
        s, q, rows = m
        return h_copy(index(s, chip, core), cx * 2 + cy, rows, hd_sem.at[K + j], d_dev)

    def pair_a(m):
        s, q, rows = m
        return h_copy(index(s, chip, core), pl.ds(cx * 2, 2), rows, ca_sem.at[lax.rem(q, K)], c_dev)

    def pair_b(m):
        s, q, rows = m
        return h_copy(index(s, 1 - chip, core), pl.ds(cxn * 2, 2), rows, cb_sem.at[lax.rem(q, K)], c_dev)

    def partial(s):
        tcx, tz, sub = token(s, chip, core)

        @pl.when((sub == 0) & (lax.rem(tcx, 2) != core))
        def _():
            xc_copy(lax.div(s, 2 * Q), tcx, tz).wait_recv()

        ps[s] = jnp.dot(xg[(tcx * 2 + tz) * Q + sub], w1v[0], preferred_element_type=jnp.float32)

    def keep(s):
        kept[...] = jnp.dot(xg[index(s, chip, core)], w1v[1], preferred_element_type=jnp.float32)

    def make_h(m):
        s, _, rows = m
        p_copy(m).wait_recv()
        c = (kept[rows] + pr[s, rows]).astype(jnp.bfloat16).astype(jnp.float32)
        hb[index(s, chip, core), cx * 2 + cy, rows] = gelu(c).astype(jnp.bfloat16)
        own_y(m).start()
        own_x(m).start()

    def products(t, xx, kk, rows):
        b = (xx * 2 + kk) * 2
        return (jnp.dot(hb[t, b, rows], w2v[b], preferred_element_type=jnp.float32)
                + jnp.dot(hb[t, b + 1, rows], w2v[b + 1], preferred_element_type=jnp.float32))

    def z_copy(t, k, rows):
        return remote(zacc.at[t, rows], zr.at[k, rows], z_send, z_sem.at[k], z_dev)

    def f_copy(tcx, sub, rows, dev):
        return remote(zo.at[tcx * Q + sub, rows], zfin.at[sub, cx, rows], f_send, f_sem, dev)

    def finish(s, xx, local, rows):
        tcx, tz, sub = token(s, xx, 1)
        t = (tcx * 2 + tz) * Q + sub
        k = tcx * Q + sub
        kind = lax.div(s, 2 * Q)
        if isinstance(s, int) and s >= 2 * Q:
            acc = zacc[t, rows] + products(t, xx, 0, rows) + products(t, xx, 1, rows)
        else:
            t0 = index(s, xx, 0)
            zacc[t0, rows] += products(t0, xx, 0, rows)
            acc = zacc[t, rows] + products(t, xx, 1, rows)

        @pl.when(kind < 3)
        def _():
            zacc[t, rows] = acc

        @pl.when(kind == 2)
        def _():
            z_copy(t, k, rows).start()

        @pl.when(kind == 3)
        def _():
            if rows.start == 0:
                z_copy(t, k, pl.ds(0, R)).wait_recv()
            z = (acc + zr[k, rows]).astype(jnp.bfloat16)
            if local:
                @pl.when(tcx == cx)
                def _():
                    zfin[sub, cx, rows] = z

                @pl.when(tcx != cx)
                def _():
                    zo[k, rows] = z
                    f_copy(tcx, sub, rows, c_dev).start()
            else:
                zo[k, rows] = z
                f_copy(tcx, sub, rows, (cz, cy, tcx)).start()

    def relay(m, ahead=True):
        own_y(m).wait_recv()
        if ahead:
            y_to_x(m).start()
        pair_a(m).start()

    def relay_far(m, j=None):
        own_x(m).wait_recv()
        if j is None:
            y_to_x(m).wait_recv()
        else:
            s, q, rows = m
            h_copy(index(s, 1 - chip, core), cxn * 2 + 1 - cy, rows, hd_sem.at[K + j], d_dev).wait_recv()
        pair_b(m).start()

    def near(s, ms, rows=pl.ds(0, R)):
        for m in ms:
            pair_a(m).wait_recv()
        finish(s, chip, False, rows)

    def far(s, ms, rows=pl.ds(0, R)):
        for m in ms:
            pair_b(m).wait_recv()
        finish(s, 1 - chip, True, rows)

    barrier = pltpu.get_barrier_semaphore()
    partners = (y_dev, z_dev, x_dev, c_dev, xc_dev)
    for dev in partners:
        pl.semaphore_signal(barrier, inc=1, device_id=dev, device_id_type=MESH)
    other = pl.multiple_of((1 - cy) * 768, 128)
    mine = pl.multiple_of(cy * 768, 128)
    x_load = pltpu.make_async_copy(x_ref, block(cx, cz), load_sem.at[0])
    send_load = pltpu.make_async_copy(w1_ref.at[:, pl.ds(other, 768)], w1v.at[0], load_sem.at[1])
    keep_load = pltpu.make_async_copy(w1_ref.at[:, pl.ds(mine, 768)], w1v.at[1], load_sem.at[2])
    w2_load = pltpu.make_async_copy(w2_ref, w2v, load_sem.at[3])
    x_load.start()
    send_load.start()
    x_load.wait()
    send_load.wait()
    keep_load.start()
    w2_load.start()

    partial(0)
    pl.semaphore_wait(barrier, len(partners))
    p_copy(whole(0)).start()
    xc_copy(0, cx, cz).start()
    x_copy(0, cx, cz, x_dev).start()
    x_copy(1, cx, cz, z_dev).start()
    zacc[...] = jnp.zeros_like(zacc)

    def body(i, _):
        partial(i + 1)
        p_copy(whole(i + 1)).start()

        @pl.when(i == 0)
        def _():
            keep_load.wait()

        keep(i)
        make_h(whole(i))

        @pl.when(i == FWD_X)
        def _():
            w2_load.wait()
            x_copy(1, cx, 1 - cz, z_dev).wait_recv()
            xc_copy(1, cx, 1 - cz).start()
            x_copy(0, cxn, cz, x_dev).wait_recv()
            x_copy(2, cxn, cz, z_dev).start()
            xc_copy(3, cxn, cz).start()

        @pl.when(i == FWD_DIAG)
        def _():
            x_copy(2, cxn, 1 - cz, z_dev).wait_recv()
            xc_copy(2, cxn, 1 - cz).start()

        @pl.when(i >= 1)
        def _():
            relay(whole(i - 1))

        @pl.when(i >= 2)
        def _():
            m = whole(i - 2)
            near(i - 2, [m])
            relay_far(m)

        @pl.when(i >= 3)
        def _():
            far(i - 3, [whole(i - 3)])

        return 0

    lax.fori_loop(0, T - 1, body, 0)

    m = pieces(T) + pieces(T + 1)
    w = {s: whole(s) for s in range(T - 4, T)}
    partial(T)
    for piece in m[:3]:
        p_copy(piece).start()
    keep(T - 1)
    make_h(w[T - 1])
    partial(T + 1)
    p_copy(m[3]).start()
    p_copy(m[4]).start()
    relay(w[T - 2])
    near(T - 3, [w[T - 3]])
    relay_far(w[T - 3])
    far(T - 4, [w[T - 4]])
    keep(T)
    make_h(m[0])
    p_copy(m[5]).start()
    near(T - 2, [w[T - 2]])
    make_h(m[1])
    far(T - 3, [w[T - 3]])
    make_h(m[2])
    relay_far(w[T - 2])
    keep(T + 1)
    relay(w[T - 1])
    far(T - 2, [w[T - 2]])
    make_h(m[3])
    near(T - 1, [w[T - 1]])
    make_h(m[4])
    own_d(m[4], 0).start()
    relay(m[0])
    make_h(m[5])
    own_d(m[5], 1).start()
    relay_far(w[T - 1])
    relay(m[1])
    relay(m[2])
    far(T - 1, [w[T - 1]])
    relay(m[3])
    near(T, m[:3])
    relay(m[4], False)
    relay(m[5], False)
    near(T + 1, m[3:5], pl.ds(0, 2 * PIECE))
    relay_far(m[0])
    near(T + 1, m[5:], pl.ds(2 * PIECE, PIECE))
    relay_far(m[1])
    relay_far(m[2])
    relay_far(m[3])
    relay_far(m[4], 0)
    relay_far(m[5], 1)
    far(T, m[:3])
    far(T + 1, m[3:])

    part = zo.at[pl.ds(0, 3 * Q)]
    pltpu.make_async_copy(part, part, f_sem).wait()
    for sub in range(Q):
        for j in range(4):
            out_ref[sub, :, j * 384:(j + 1) * 384] = zfin[sub, j]

    sent = xg.at[pl.ds(0, 7 * Q)]
    pltpu.make_async_copy(sent, sent, x_send).wait()
    pltpu.make_async_copy(ps, pr, p_send).wait()
    sent = hb.at[:, pl.ds(0, 7)]
    pltpu.make_async_copy(sent, sent, h_send).wait()
    pltpu.make_async_copy(zr, zr, z_send).wait()
    pltpu.make_async_copy(part, part, f_send).wait()


def solution(mesh):
    def body(x, w1, w2):
        bf16, f32 = jnp.bfloat16, jnp.float32
        dma = pltpu.SemaphoreType.DMA
        inputs = (x.reshape(Q, R, 1536), w1, w2.reshape(8, 768, 384))
        out = pl.pallas_call(
            kernel,
            out_shape=jax.ShapeDtypeStruct((Q, R, 1536), bf16),
            in_specs=[pl.BlockSpec(memory_space=pltpu.HBM)] * 3,
            out_specs=pl.BlockSpec(memory_space=pltpu.VMEM),
            scratch_shapes=[
                pltpu.VMEM((S, R, 1536), bf16),
                pltpu.VMEM((2, 1536, 768), bf16),
                pltpu.VMEM((8, 768, 384), bf16),
                pltpu.VMEM((S, R, 768), f32),
                pltpu.VMEM((S, R, 768), f32),
                pltpu.VMEM((R, 768), f32),
                pltpu.VMEM((S, 8, R, 768), bf16),
                pltpu.VMEM((S, R, 384), f32),
                pltpu.VMEM((4 * Q, R, 384), f32),
                pltpu.VMEM((4 * Q, R, 384), bf16),
                pltpu.VMEM((Q, 4, R, 384), bf16),
                dma((4,)), dma(()), dma((3,)), dma((4,)), dma(()), dma((K,)), dma(()), dma((K,)), dma((KX,)),
                dma((K + 2,)), dma((K,)), dma((K,)), dma(()), dma((4 * Q,)), dma(()), dma(()),
            ],
            compiler_params=pltpu.CompilerParams(
                collective_id=0, has_side_effects=True, vmem_limit_bytes=40 * 2**20),
        )(*(pltpu.with_memory_space_constraint(v, pltpu.HBM) for v in inputs))
        return out.reshape(96, 1536)

    return jax.shard_map(
        body,
        mesh=mesh,
        in_specs=(P(("cx", "cz"), "cy"), P("cy", ("cz", "cx")), P("cz", ("cy", "cx"))),
        out_specs=P(("cx", "cz"), "cy"),
        check_vma=False,
    )
```

time: 91.4 us -> 89.8 us (0.982)
  Pallas kernels: 90.5 us -> 88.9 us
    pallas_call x1, Pallas kernels: 90.5 us -> 88.9 us  [body(): pl.pallas_call(kernel, out_shape=jax.ShapeDtypeStruct((Q, R, 1536), bf16)...]
where the time goes in v3:
time: 89.8 us; the launch traced here: 89.7 us
  Pallas kernels  88.9 us (99%)
    pallas_call x1, Pallas kernels, body(): pl.pallas_call(kernel, out_shape=jax.ShapeDtypeStruct((Q, R, 1536), bf16)...  88.9 us

profile of v3, /device:TPU:0, one launch (start us, length us, event | category | flops | bytes accessed | tf_op | source)
XLA Modules:
  0.0 89.7 jit_solution(5012231040711868124)
XLA Ops:
  0.0 88.9 %shard_map.37 = bf16[2,48,1536]{2,1,0:T(8,128)(2,1)S(1)} custom-call(bf16[2,48,1536]{2,1,0:T(8,128)(2,1)} %bitcast.5, bf16[1536,1536]{1,0:T(8,128)(2,1)} %w1_ref.1, bf16[8,768,384]{2,1,0:T(8,128)(2,1)} %bitcast.4), custom_call_target="tpu_custom_call" | custom-call | tf_op jit(solution)/shard_map/pallas_call | solution.py:337
  88.9 0.7 copy.5

commit v4 on v3

--- a/solution.py
+++ b/solution.py
@@ -43,16 +43,23 @@
         return pltpu.make_async_remote_copy(
             src_ref=src, dst_ref=dst, send_sem=send, recv_sem=recv, device_id=dev, device_id_type=MESH)
 
+    def apart(f):
+        def run(*args):
+            @pl.when(cx >= 0)
+            def _():
+                f(*args)
+        return run
+
     def token(s, xx, kk):
         seg, sub = lax.div(s, Q), lax.rem(s, Q)
-        kind = lax.div(seg, 2)
+        kind = jnp.where(seg < 4, lax.div(seg, 2), 2 + lax.rem(seg, 2))
         tx = jnp.where(kind < 2, xx, 1 - xx)
         tz = jnp.where((kind == 0) | (kind == 3), cz, 1 - cz)
-        tcx = 2 * tx + jnp.where(kind == 0, lax.rem(seg + kk, 2), lax.rem(seg, 2))
-        return tcx, tz, sub
+        half = jnp.where(kind == 0, lax.rem(seg + kk, 2), jnp.where(kind == 1, lax.rem(seg, 2), lax.rem(lax.div(seg, 2), 2)))
+        return 2 * tx + half, tz, sub, kind
 
     def index(s, xx, kk):
-        tcx, tz, sub = token(s, xx, kk)
+        tcx, tz, sub, _ = token(s, xx, kk)
         return (tcx * 2 + tz) * Q + sub
 
     def block(tcx, tz):
@@ -101,18 +108,21 @@
         s, q, rows = m
         return h_copy(index(s, 1 - chip, core), pl.ds(cxn * 2, 2), rows, cb_sem.at[lax.rem(q, K)], c_dev)
 
+    @apart
     def partial(s):
-        tcx, tz, sub = token(s, chip, core)
+        tcx, tz, sub, kind = token(s, chip, core)
 
         @pl.when((sub == 0) & (lax.rem(tcx, 2) != core))
         def _():
-            xc_copy(lax.div(s, 2 * Q), tcx, tz).wait_recv()
+            xc_copy(kind, tcx, tz).wait_recv()
 
         ps[s] = jnp.dot(xg[(tcx * 2 + tz) * Q + sub], w1v[0], preferred_element_type=jnp.float32)
 
+    @apart
     def keep(s):
         kept[...] = jnp.dot(xg[index(s, chip, core)], w1v[1], preferred_element_type=jnp.float32)
 
+    @apart
     def make_h(m):
         s, _, rows = m
         p_copy(m).wait_recv()
@@ -132,11 +142,11 @@
     def f_copy(tcx, sub, rows, dev):
         return remote(zo.at[tcx * Q + sub, rows], zfin.at[sub, cx, rows], f_send, f_sem, dev)
 
+    @apart
     def finish(s, xx, local, rows):
-        tcx, tz, sub = token(s, xx, 1)
+        tcx, tz, sub, kind = token(s, xx, 1)
         t = (tcx * 2 + tz) * Q + sub
         k = tcx * Q + sub
-        kind = lax.div(s, 2 * Q)
         if isinstance(s, int) and s >= 2 * Q:
             acc = zacc[t, rows] + products(t, xx, 0, rows) + products(t, xx, 1, rows)
         else:
@@ -170,12 +180,14 @@
                 zo[k, rows] = z
                 f_copy(tcx, sub, rows, (cz, cy, tcx)).start()
 
+    @apart
     def relay(m, ahead=True):
         own_y(m).wait_recv()
         if ahead:
             y_to_x(m).start()
         pair_a(m).start()
 
+    @apart
     def relay_far(m, j=None):
         own_x(m).wait_recv()
         if j is None:
@@ -202,19 +214,25 @@
     other = pl.multiple_of((1 - cy) * 768, 128)
     mine = pl.multiple_of(cy * 768, 128)
     x_load = pltpu.make_async_copy(x_ref, block(cx, cz), load_sem.at[0])
-    send_load = pltpu.make_async_copy(w1_ref.at[:, pl.ds(other, 768)], w1v.at[0], load_sem.at[1])
-    keep_load = pltpu.make_async_copy(w1_ref.at[:, pl.ds(mine, 768)], w1v.at[1], load_sem.at[2])
-    w2_load = pltpu.make_async_copy(w2_ref, w2v, load_sem.at[3])
+    send_loads = [
+        pltpu.make_async_copy(
+            w1_ref.at[:, pl.ds(other + j * 256, 256)], w1v.at[0, :, pl.ds(j * 256, 256)], load_sem.at[1 + j])
+        for j in range(3)]
+    keep_load = pltpu.make_async_copy(w1_ref.at[:, pl.ds(mine, 768)], w1v.at[1], load_sem.at[4])
+    w2_load = pltpu.make_async_copy(w2_ref, w2v, load_sem.at[5])
     x_load.start()
-    send_load.start()
+    for load in send_loads:
+        load.start()
     x_load.wait()
-    send_load.wait()
+    for j, load in enumerate(send_loads):
+        load.wait()
+        cols = pl.ds(j * 256, 256)
+        ps[0, :, cols] = jnp.dot(xg[index(0, chip, core)], w1v[0, :, cols], preferred_element_type=jnp.float32)
+        if j == 0:
+            pl.semaphore_wait(barrier, len(partners))
+        remote(ps.at[0, :, cols], pr.at[0, :, cols], p_send, p_sem.at[0], y_dev).start()
     keep_load.start()
     w2_load.start()
-
-    partial(0)
-    pl.semaphore_wait(barrier, len(partners))
-    p_copy(whole(0)).start()
     xc_copy(0, cx, cz).start()
     x_copy(0, cx, cz, x_dev).start()
     x_copy(1, cx, cz, z_dev).start()
@@ -351,7 +369,7 @@
                 pltpu.VMEM((4 * Q, R, 384), f32),
                 pltpu.VMEM((4 * Q, R, 384), bf16),
                 pltpu.VMEM((Q, 4, R, 384), bf16),
-                dma((4,)), dma(()), dma((3,)), dma((4,)), dma(()), dma((K,)), dma(()), dma((K,)), dma((KX,)),
+                dma((6,)), dma(()), dma((3,)), dma((4,)), dma(()), dma((K,)), dma(()), dma((K,)), dma((KX,)),
                 dma((K + 2,)), dma((K,)), dma((K,)), dma(()), dma((4 * Q,)), dma(()), dma(()),
             ],
             compiler_params=pltpu.CompilerParams(

time: 89.8 us -> 88.4 us (0.984)
  Pallas kernels: 88.9 us -> 87.6 us
    pallas_call x1, Pallas kernels: 88.9 us -> 87.6 us  [body(): pl.pallas_call(kernel, out_shape=jax.ShapeDtypeStruct((Q, R, 1536), bf16)...]
where the time goes in v4:
time: 88.4 us; the launch traced here: 88.3 us
  Pallas kernels  87.6 us (99%)
    pallas_call x1, Pallas kernels, body(): pl.pallas_call(kernel, out_shape=jax.ShapeDtypeStruct((Q, R, 1536), bf16)...  87.6 us

profile of v4, /device:TPU:0, one launch (start us, length us, event | category | flops | bytes accessed | tf_op | source)
XLA Modules:
  0.0 88.3 jit_solution(7047214909884020859)
XLA Ops:
  0.0 87.6 %shard_map.37 = bf16[2,48,1536]{2,1,0:T(8,128)(2,1)S(1)} custom-call(bf16[2,48,1536]{2,1,0:T(8,128)(2,1)} %bitcast.5, bf16[1536,1536]{1,0:T(8,128)(2,1)} %w1_ref.1, bf16[8,768,384]{2,1,0:T(8,128)(2,1)} %bitcast.4), custom_call_target="tpu_custom_call" | custom-call | tf_op jit(solution)/shard_map/pallas_call | solution.py:355
  87.6 0.7 copy.5

commit v5 on v4

--- a/solution.py
+++ b/solution.py
@@ -16,6 +16,7 @@
 N = R // PIECE
 K = 8
 KX = 10
+KB = 4
 FWD_X = 1
 FWD_DIAG = 2 * Q
 
@@ -106,7 +107,7 @@
 
     def pair_b(m):
         s, q, rows = m
-        return h_copy(index(s, 1 - chip, core), pl.ds(cxn * 2, 2), rows, cb_sem.at[lax.rem(q, K)], c_dev)
+        return h_copy(index(s, 1 - chip, core), pl.ds(cxn * 2, 2), rows, cb_sem.at[lax.rem(q, KB)], c_dev)
 
     @apart
     def partial(s):
@@ -141,6 +142,23 @@
 
     def f_copy(tcx, sub, rows, dev):
         return remote(zo.at[tcx * Q + sub, rows], zfin.at[sub, cx, rows], f_send, f_sem, dev)
+
+    def deliver(acc, t, tcx, sub, k, local, rows):
+        if rows.start == 0:
+            z_copy(t, k, pl.ds(0, R)).wait_recv()
+        z = (acc + zr[k, rows]).astype(jnp.bfloat16)
+        if local:
+            @pl.when(tcx == cx)
+            def _():
+                zfin[sub, cx, rows] = z
+
+            @pl.when(tcx != cx)
+            def _():
+                zo[k, rows] = z
+                f_copy(tcx, sub, rows, c_dev).start()
+        else:
+            zo[k, rows] = z
+            f_copy(tcx, sub, rows, (cz, cy, tcx)).start()
 
     @apart
     def finish(s, xx, local, rows):
@@ -164,21 +182,7 @@
 
         @pl.when(kind == 3)
         def _():
-            if rows.start == 0:
-                z_copy(t, k, pl.ds(0, R)).wait_recv()
-            z = (acc + zr[k, rows]).astype(jnp.bfloat16)
-            if local:
-                @pl.when(tcx == cx)
-                def _():
-                    zfin[sub, cx, rows] = z
-
-                @pl.when(tcx != cx)
-                def _():
-                    zo[k, rows] = z
-                    f_copy(tcx, sub, rows, c_dev).start()
-            else:
-                zo[k, rows] = z
-                f_copy(tcx, sub, rows, (cz, cy, tcx)).start()
+            deliver(acc, t, tcx, sub, k, local, rows)
 
     @apart
     def relay(m, ahead=True):
@@ -188,14 +192,56 @@
         pair_a(m).start()
 
     @apart
-    def relay_far(m, j=None):
+    def relay_far(m):
         own_x(m).wait_recv()
+        y_to_x(m).wait_recv()
+        pair_b(m).start()
+
+    def single(m, yy):
+        s, _, rows = m
+        which = KB + 2 * (s - T) + jnp.where(yy == cy, 0, 1)
+        return h_copy(index(s, 1 - chip, core), cxn * 2 + yy, rows, cb_sem.at[which], c_dev)
+
+    @apart
+    def relay_x(m):
+        own_x(m).wait_recv()
+        single(m, cy).start()
+
+    @apart
+    def relay_diag(m, j=None):
         if j is None:
             y_to_x(m).wait_recv()
         else:
             s, q, rows = m
             h_copy(index(s, 1 - chip, core), cxn * 2 + 1 - cy, rows, hd_sem.at[K + j], d_dev).wait_recv()
-        pair_b(m).start()
+        single(m, 1 - cy).start()
+
+    @apart
+    def far_half(yy, final):
+        for s in (T, T + 1):
+            single((s, s, pl.ds(0, R)), yy).wait_recv()
+        tcx, tz, _, _ = token(T, 1 - chip, 1)
+        k, first, b = tcx * Q, (tcx * 2 + tz) * Q, (1 - chip) * 4 + yy
+        t = pl.ds(first, Q)
+        h0, h1 = hb[t, b].reshape(Q * R, 768), hb[t, b + 2].reshape(Q * R, 768)
+        acc = zacc[t].reshape(Q * R, 384) + (
+            jnp.dot(h0, w2v[b], preferred_element_type=jnp.float32)
+            + jnp.dot(h1, w2v[b + 2], preferred_element_type=jnp.float32))
+        if not final:
+            zacc[t] = acc.reshape(Q, R, 384)
+            return
+        for sub in range(Q):
+            z_copy(first + sub, k + sub, pl.ds(0, R)).wait_recv()
+        z = (acc + zr[pl.ds(k, Q)].reshape(Q * R, 384)).astype(jnp.bfloat16).reshape(Q, R, 384)
+
+        @pl.when(tcx == cx)
+        def _():
+            zfin[:, cx] = z
+
+        @pl.when(tcx != cx)
+        def _():
+            zo[pl.ds(k, Q)] = z
+            remote(zo.at[pl.ds(k, Q)], zfin.at[:, cx], f_send, f_sem, c_dev).start()
 
     def near(s, ms, rows=pl.ds(0, R)):
         for m in ms:
@@ -309,28 +355,58 @@
     make_h(m[3])
     near(T - 1, [w[T - 1]])
     make_h(m[4])
-    own_d(m[4], 0).start()
     relay(m[0])
     make_h(m[5])
+    own_d(m[4], 0).start()
     own_d(m[5], 1).start()
     relay_far(w[T - 1])
+
+    @pl.when(core == 0)
+    def _():
+        far(T - 1, [w[T - 1]])
+
     relay(m[1])
     relay(m[2])
-    far(T - 1, [w[T - 1]])
-    relay(m[3])
-    near(T, m[:3])
-    relay(m[4], False)
-    relay(m[5], False)
-    near(T + 1, m[3:5], pl.ds(0, 2 * PIECE))
-    relay_far(m[0])
-    near(T + 1, m[5:], pl.ds(2 * PIECE, PIECE))
-    relay_far(m[1])
-    relay_far(m[2])
-    relay_far(m[3])
-    relay_far(m[4], 0)
-    relay_far(m[5], 1)
-    far(T, m[:3])
-    far(T + 1, m[3:])
+
+    @pl.when(core == 0)
+    def _():
+        relay(m[3])
+        near(T, m[:3])
+        relay(m[4], False)
+        relay(m[5], False)
+        near(T + 1, m[3:5], pl.ds(0, 2 * PIECE))
+        near(T + 1, m[5:], pl.ds(2 * PIECE, PIECE))
+        for piece in m:
+            relay_x(piece)
+        relay_diag(m[0])
+        far_half(cy, False)
+        relay_diag(m[1])
+        relay_diag(m[2])
+        relay_diag(m[3])
+        relay_diag(m[4], 0)
+        relay_diag(m[5], 1)
+        far_half(1 - cy, True)
+
+
+    @pl.when(core == 1)
+    def _():
+        relay(m[3])
+        relay(m[4], False)
+        relay(m[5], False)
+        far(T - 1, [w[T - 1]])
+        near(T, m[:3])
+        for piece in m:
+            relay_x(piece)
+        relay_diag(m[0])
+        relay_diag(m[1])
+        relay_diag(m[2])
+        relay_diag(m[3])
+        near(T + 1, m[3:5], pl.ds(0, 2 * PIECE))
+        relay_diag(m[4], 0)
+        relay_diag(m[5], 1)
+        near(T + 1, m[5:], pl.ds(2 * PIECE, PIECE))
+        far_half(cy, False)
+        far_half(1 - cy, True)
 
     part = zo.at[pl.ds(0, 3 * Q)]
     pltpu.make_async_copy(part, part, f_sem).wait()
@@ -370,7 +446,7 @@
                 pltpu.VMEM((4 * Q, R, 384), bf16),
                 pltpu.VMEM((Q, 4, R, 384), bf16),
                 dma((6,)), dma(()), dma((3,)), dma((4,)), dma(()), dma((K,)), dma(()), dma((K,)), dma((KX,)),
-                dma((K + 2,)), dma((K,)), dma((K,)), dma(()), dma((4 * Q,)), dma(()), dma(()),
+                dma((K + 2,)), dma((K,)), dma((KB + 4,)), dma(()), dma((4 * Q,)), dma(()), dma(()),
             ],
             compiler_params=pltpu.CompilerParams(
                 collective_id=0, has_side_effects=True, vmem_limit_bytes=40 * 2**20),

time: 88.4 us -> 87.4 us (0.989)
  Pallas kernels: 87.6 us -> 86.6 us
    pallas_call x1, Pallas kernels: 87.6 us -> 86.6 us  [body(): pl.pallas_call(kernel, out_shape=jax.ShapeDtypeStruct((Q, R, 1536), bf16)...]
where the time goes in v5:
time: 87.4 us; the launch traced here: 87.3 us
  Pallas kernels  86.6 us (99%)
    pallas_call x1, Pallas kernels, body(): pl.pallas_call(kernel, out_shape=jax.ShapeDtypeStruct((Q, R, 1536), bf16)...  86.6 us

profile of v5, /device:TPU:0, one launch (start us, length us, event | category | flops | bytes accessed | tf_op | source)
XLA Modules:
  0.0 87.3 jit_solution(7537111586969651492)
XLA Ops:
  0.0 86.6 %shard_map.37 = bf16[2,48,1536]{2,1,0:T(8,128)(2,1)S(1)} custom-call(bf16[2,48,1536]{2,1,0:T(8,128)(2,1)} %bitcast.5, bf16[1536,1536]{1,0:T(8,128)(2,1)} %w1_ref.1, bf16[8,768,384]{2,1,0:T(8,128)(2,1)} %bitcast.4), custom_call_target="tpu_custom_call" | custom-call | tf_op jit(solution)/shard_map/pallas_call | solution.py:431
  86.6 0.7 copy.5

commit v6 on v5

--- a/solution.py
+++ b/solution.py
@@ -357,8 +357,12 @@
     make_h(m[4])
     relay(m[0])
     make_h(m[5])
-    own_d(m[4], 0).start()
-    own_d(m[5], 1).start()
+
+    @pl.when(core == 0)
+    def _():
+        own_d(m[4], 0).start()
+        own_d(m[5], 1).start()
+
     relay_far(w[T - 1])
 
     @pl.when(core == 0)
@@ -391,8 +395,8 @@
     @pl.when(core == 1)
     def _():
         relay(m[3])
-        relay(m[4], False)
-        relay(m[5], False)
+        relay(m[4])
+        relay(m[5])
         far(T - 1, [w[T - 1]])
         near(T, m[:3])
         for piece in m:
@@ -402,8 +406,8 @@
         relay_diag(m[2])
         relay_diag(m[3])
         near(T + 1, m[3:5], pl.ds(0, 2 * PIECE))
-        relay_diag(m[4], 0)
-        relay_diag(m[5], 1)
+        relay_diag(m[4])
+        relay_diag(m[5])
         near(T + 1, m[5:], pl.ds(2 * PIECE, PIECE))
         far_half(cy, False)
         far_half(1 - cy, True)

time: 87.4 us -> 87.3 us (level)
  no operation moved by 1% of the time
where the time goes in v6:
time: 87.3 us; the launch traced here: 87.2 us
  Pallas kernels  86.5 us (99%)
    pallas_call x1, Pallas kernels, body(): pl.pallas_call(kernel, out_shape=jax.ShapeDtypeStruct((Q, R, 1536), bf16)...  86.5 us

profile of v6, /device:TPU:0, one launch (start us, length us, event | category | flops | bytes accessed | tf_op | source)
XLA Modules:
  0.0 87.2 jit_solution(1269085004926146002)
XLA Ops:
  0.0 86.5 %shard_map.37 = bf16[2,48,1536]{2,1,0:T(8,128)(2,1)S(1)} custom-call(bf16[2,48,1536]{2,1,0:T(8,128)(2,1)} %bitcast.5, bf16[1536,1536]{1,0:T(8,128)(2,1)} %w1_ref.1, bf16[8,768,384]{2,1,0:T(8,128)(2,1)} %bitcast.4), custom_call_target="tpu_custom_call" | custom-call | tf_op jit(solution)/shard_map/pallas_call | solution.py:435
  86.5 0.7 copy.5

commit v7 on v6

--- a/solution.py
+++ b/solution.py
@@ -15,6 +15,7 @@
 PIECE = 16
 N = R // PIECE
 K = 8
+KP = 7
 KX = 10
 KB = 4
 FWD_X = 1
@@ -80,14 +81,14 @@
 
     def p_copy(m):
         s, q, rows = m
-        return remote(ps.at[s, rows], pr.at[s, rows], p_send, p_sem.at[lax.rem(q, K)], y_dev)
+        return remote(ps.at[s, rows], pr.at[s, rows], p_send, p_sem.at[lax.rem(q, KP)], y_dev)
 
     def h_copy(t, b, rows, recv, dev):
         return remote(hb.at[t, b, rows], hb.at[t, b, rows], h_send, recv, dev)
 
     def own_y(m):
         s, q, rows = m
-        return h_copy(index(s, chip, core), cx * 2 + cy, rows, hy_sem.at[lax.rem(q, K)], y_dev)
+        return h_copy(index(s, chip, core), cx * 2 + cy, rows, hy_sem.at[lax.rem(q, KP)], y_dev)
 
     def own_x(m):
         s, q, rows = m
@@ -103,7 +104,7 @@
 
     def pair_a(m):
         s, q, rows = m
-        return h_copy(index(s, chip, core), pl.ds(cx * 2, 2), rows, ca_sem.at[lax.rem(q, K)], c_dev)
+        return h_copy(index(s, chip, core), pl.ds(cx * 2, 2), rows, ca_sem.at[lax.rem(q, KP)], c_dev)
 
     def pair_b(m):
         s, q, rows = m
@@ -264,8 +265,8 @@
         pltpu.make_async_copy(
             w1_ref.at[:, pl.ds(other + j * 256, 256)], w1v.at[0, :, pl.ds(j * 256, 256)], load_sem.at[1 + j])
         for j in range(3)]
-    keep_load = pltpu.make_async_copy(w1_ref.at[:, pl.ds(mine, 768)], w1v.at[1], load_sem.at[4])
-    w2_load = pltpu.make_async_copy(w2_ref, w2v, load_sem.at[5])
+    keep_load = pltpu.make_async_copy(w1_ref.at[:, pl.ds(mine, 768)], w1v.at[1], load_sem.at[0])
+    w2_load = pltpu.make_async_copy(w2_ref, w2v, load_sem.at[1])
     x_load.start()
     for load in send_loads:
         load.start()
@@ -449,8 +450,8 @@
                 pltpu.VMEM((4 * Q, R, 384), f32),
                 pltpu.VMEM((4 * Q, R, 384), bf16),
                 pltpu.VMEM((Q, 4, R, 384), bf16),
-                dma((6,)), dma(()), dma((3,)), dma((4,)), dma(()), dma((K,)), dma(()), dma((K,)), dma((KX,)),
-                dma((K + 2,)), dma((K,)), dma((KB + 4,)), dma(()), dma((4 * Q,)), dma(()), dma(()),
+                dma((4,)), dma(()), dma((3,)), dma((4,)), dma(()), dma((KP,)), dma(()), dma((KP,)), dma((KX,)),
+                dma((K + 2,)), dma((KP,)), dma((KB + 4,)), dma(()), dma((4 * Q,)), dma(()), dma(()),
             ],
             compiler_params=pltpu.CompilerParams(
                 collective_id=0, has_side_effects=True, vmem_limit_bytes=40 * 2**20),

time: 87.3 us -> 87.3 us (level)
  no operation moved by 1% of the time
where the time goes in v7:
time: 87.3 us; the launch traced here: 87.2 us
  Pallas kernels  86.5 us (99%)
    pallas_call x1, Pallas kernels, body(): pl.pallas_call(kernel, out_shape=jax.ShapeDtypeStruct((Q, R, 1536), bf16)...  86.5 us

profile of v7, /device:TPU:0, one launch (start us, length us, event | category | flops | bytes accessed | tf_op | source)
XLA Modules:
  0.0 87.2 jit_solution(18050292088725823688)
XLA Ops:
  0.0 86.5 %shard_map.37 = bf16[2,48,1536]{2,1,0:T(8,128)(2,1)S(1)} custom-call(bf16[2,48,1536]{2,1,0:T(8,128)(2,1)} %bitcast.5, bf16[1536,1536]{1,0:T(8,128)(2,1)} %w1_ref.1, bf16[8,768,384]{2,1,0:T(8,128)(2,1)} %bitcast.4), custom_call_target="tpu_custom_call" | custom-call | tf_op jit(solution)/shard_map/pallas_call | solution.py:436
  86.5 0.7 copy.5

commit v8 on v7

--- a/solution.py
+++ b/solution.py
@@ -14,10 +14,9 @@
 T = S - 2
 PIECE = 16
 N = R // PIECE
-K = 8
 KP = 7
 KX = 10
-KB = 4
+KB = 3
 FWD_X = 1
 FWD_DIAG = 2 * Q
 
@@ -96,11 +95,11 @@
 
     def y_to_x(m):
         s, q, rows = m
-        return h_copy(index(s, chip, core), cx * 2 + 1 - cy, rows, hd_sem.at[lax.rem(q, K)], x_dev)
+        return h_copy(index(s, chip, core), cx * 2 + 1 - cy, rows, hd_sem.at[lax.rem(q, KP)], x_dev)
 
     def own_d(m, j):
         s, q, rows = m
-        return h_copy(index(s, chip, core), cx * 2 + cy, rows, hd_sem.at[K + j], d_dev)
+        return h_copy(index(s, chip, core), cx * 2 + cy, rows, hd_sem.at[KP + j], d_dev)
 
     def pair_a(m):
         s, q, rows = m
@@ -214,7 +213,7 @@
             y_to_x(m).wait_recv()
         else:
             s, q, rows = m
-            h_copy(index(s, 1 - chip, core), cxn * 2 + 1 - cy, rows, hd_sem.at[K + j], d_dev).wait_recv()
+            h_copy(index(s, 1 - chip, core), cxn * 2 + 1 - cy, rows, hd_sem.at[KP + j], d_dev).wait_recv()
         single(m, 1 - cy).start()
 
     @apart
@@ -451,7 +450,7 @@
                 pltpu.VMEM((4 * Q, R, 384), bf16),
                 pltpu.VMEM((Q, 4, R, 384), bf16),
                 dma((4,)), dma(()), dma((3,)), dma((4,)), dma(()), dma((KP,)), dma(()), dma((KP,)), dma((KX,)),
-                dma((K + 2,)), dma((KP,)), dma((KB + 4,)), dma(()), dma((4 * Q,)), dma(()), dma(()),
+                dma((KP + 2,)), dma((KP,)), dma((KB + 4,)), dma(()), dma((4 * Q,)), dma(()), dma(()),
             ],
             compiler_params=pltpu.CompilerParams(
                 collective_id=0, has_side_effects=True, vmem_limit_bytes=40 * 2**20),

time: 87.3 us -> 87.3 us (level)
  no operation moved by 1% of the time
where the time goes in v8:
time: 87.3 us; the launch traced here: 87.2 us
  Pallas kernels  86.4 us (99%)
    pallas_call x1, Pallas kernels, body(): pl.pallas_call(kernel, out_shape=jax.ShapeDtypeStruct((Q, R, 1536), bf16)...  86.4 us

profile of v8, /device:TPU:0, one launch (start us, length us, event | category | flops | bytes accessed | tf_op | source)
XLA Modules:
  0.0 87.2 jit_solution(5702232644779587772)
XLA Ops:
  0.0 86.4 %shard_map.37 = bf16[2,48,1536]{2,1,0:T(8,128)(2,1)S(1)} custom-call(bf16[2,48,1536]{2,1,0:T(8,128)(2,1)} %bitcast.5, bf16[1536,1536]{1,0:T(8,128)(2,1)} %w1_ref.1, bf16[8,768,384]{2,1,0:T(8,128)(2,1)} %bitcast.4), custom_call_target="tpu_custom_call" | custom-call | tf_op jit(solution)/shard_map/pallas_call | solution.py:435
  86.4 0.7 copy.5
